TPU v7x, 256 devices: a whole 4x4x8 slice. The times are simulated.
256 devices in a mesh: dp: 16 (over y, x), sp: 8 (over z), shift: 2 (over core).
Axes of the slice: x: 4, y: 4, z: 8, core: 2. Of those that a mesh axis runs over, the one named last changes fastest.
Arguments:
- query_rows: bfloat16 [32, 2048, 32, 128], P(('shift', 'dp'), 'sp'), parts along dimension 0, may hold values from -6 to 6
- key_rows: bfloat16 [32, 2048, 32, 128], P(('shift', 'dp'), 'sp'), parts along dimension 0, may hold values from -6 to 6
- value_rows: bfloat16 [32, 2048, 32, 128], P(('shift', 'dp'), 'sp'), parts along dimension 0, may hold values from -6 to 6
- out_weight: bfloat16 [8192, 4096], P(('shift', 'dp')), parts along dimension 0, may hold values from -0.09375 to 0.09375
Outputs:
- mixer_out: bfloat16 [32, 2048, 4096], P(('shift', 'dp'), 'sp'), parts along dimension 0
There are 2 independent parts, one for each index of `shift`. A program takes and returns all parts, laid end to end along the dimension named above; each array names one. Nothing has to cross between parts.
All inputs are finite; a program needn't handle non-finite values.
Results may differ from a plain program's by a relative error of at most 0.006.
Values may be sent and summed in bfloat16 or wider, within the bound.
A program may use at most 128 MiB of HBM per device.

v0:
```python
import jax
import jax.numpy as jnp
from jax import lax
from jax.sharding import PartitionSpec as P


def feature_map(values):
    wide = values.astype(jnp.float32)
    return jnp.where(wide > 0.0, wide + 1.0, jnp.exp(jnp.minimum(wide, 0.0))).astype(jnp.bfloat16)


def finish_heads(read, count):
    result = read * count**0.5
    return result.astype(jnp.bfloat16)


def ask_state(features, state, mass):
    top = jnp.einsum(
        "bthd,bhde->bthe", features, state.astype(jnp.bfloat16), preferred_element_type=jnp.float32
    )
    bottom = jnp.einsum(
        "bthd,bhd->bth", features.astype(jnp.float32), mass, precision=lax.Precision.HIGHEST
    )
    return top / (bottom + 0.001)[..., None]


def body(query_rows, key_rows, value_rows, out_weight):
    query_feature, key_feature = (feature_map(query_rows), feature_map(key_rows))
    count = query_rows.shape[1] * lax.axis_size("sp")
    part_state = jnp.einsum(
        "bthd,bthe->bhde", key_feature, value_rows, preferred_element_type=jnp.float32
    )
    part_mass = jnp.sum(key_feature.astype(jnp.float32), axis=1)
    state, mass = lax.psum((part_state, part_mass), "sp")
    read = ask_state(query_feature, state / count, mass / count)
    mixed = finish_heads(read, count)
    mixed = mixed.reshape(mixed.shape[0], mixed.shape[1], -1)
    return jnp.einsum(
        "btw,wv->btv",
        mixed,
        lax.all_gather(out_weight, "dp", axis=0, tiled=True),
        preferred_element_type=jnp.float32,
    ).astype(jnp.bfloat16)


def solution(mesh):
    placed = (
        P(("shift", "dp"), "sp", None, None),
        P(("shift", "dp"), "sp", None, None),
        P(("shift", "dp"), "sp", None, None),
        P(("shift", "dp"), None),
    )
    return jax.shard_map(
        body, mesh=mesh, in_specs=placed, out_specs=P(("shift", "dp"), "sp", None), check_vma=False
    )
```

profile of v0, /device:TPU:2, one launch (start us, length us, event | category | flops | bytes accessed | tf_op | source)
XLA Modules:
  0.0 245.2 jit_solution(8136283110599534945)
XLA Ops:
  7.4 0.0 copy-start
  7.4 0.0 all-reduce.2.cloned.1.call-start
  7.4 3.0 %fusion.21 = (bf16[256,32,128]{2,1,0:T(8,128)(2,1)S(1)}, f32[32,128]{1,0:T(8,128)S(1)}) fusion(bf16[1,256,32,128]{3,2,1,0:T(8,128)(2,1)} %param.5), kind=kLoop, calls=%fused_computation.26 | loop fusion | flops 8384512 | bytes 4210688 | tf_op jit(solution)/shard_map/reshape
  10.3 0.0 copy-done
  10.3 3.0 %fusion.13 = f32[1,32,128,128]{3,2,1,0:T(8,128)} fusion(bf16[256,32,128]{2,1,0:T(8,128)(2,1)S(1)} %bitcast.41, bf16[256,32,128]{2,1,0:T(8,128)(2,1)S(1)} %get-tuple-element.5), kind=kOutput, calls=%fused_computation.23 | convolution fusion | flops 268435456 | bytes 6291456 | tf_op jit(solution)/shard_map/bthd,bthe->bhde/dot_general | solution.py:30
  13.4 0.0 all-reduce.2.cloned.1.call-update
  13.4 0.0 all-gather.2.cloned.1.call-start
  13.4 0.5 all-gather.2.cloned.1.call-update
  14.0 4.0 %fusion.9 = bf16[256,32,128]{2,1,0:T(8,128)(2,1)} fusion(bf16[1,256,32,128]{3,2,1,0:T(8,128)(2,1)} %param.4), kind=kLoop, calls=%fused_computation.18 | loop fusion | flops 6291456 | bytes 4194304 | tf_op jit(solution)/shard_map/reshape.5
  18.0 4.3 %copy.11 = bf16[256,32,128]{0,2,1:T(8,128)(2,1)} copy(bf16[256,32,128]{2,1,0:T(8,128)(2,1)} %fusion.9) | data formatting | bytes 4194304 | tf_op jit(solution)/shard_map/reshape.5
  22.3 32.7 %psum.15 = f32[1,32,128]{2,1,0:T(8,128)S(1)} all-reduce(f32[1,32,128]{2,1,0:T(8,128)S(1)} %bitcast.43), channel_id=1, replica_groups=mesh['dp'=16,'sp'=8,'shift'=2] {'sp'}, use_global_device_ids=true, to_apply=%region_2.3 | all-reduce | flops 4096 | bytes 32768 | tf_op jit(solution)/shard_map/psum | solution.py:34
  55.0 2.5 %fusion.24 = f32[32,1,256]{2,1,0:T(1,128)S(1)} fusion(f32[32,128,1]{1,2,0:T(1,128)S(1)} %bitcast.44, bf16[256,32,128]{0,2,1:T(8,128)(2,1)} %copy.11), kind=kOutput, calls=%fused_computation.31 | convolution fusion | flops 12582912 | bytes 2146304 | tf_op jit(solution)/shard_map/bthd,bhd->bth/dot_general | solution.py:21
  57.6 41.1 %all-reduce.2.cloned.1.call-done = f32[1,32,128,128]{3,2,1,0:T(8,128)} async-done(((f32[1,32,128,128]{3,2,1,0:T(8,128)}), f32[1,32,128,128]{3,2,1,0:T(8,128)}) %all-reduce.2.cloned.1.call-update) | async-done | bytes 2097168 | tf_op jit(solution)/shard_map/psum | solution.py:34
  98.7 4.5 %fusion.8 = bf16[1,256,32,128]{1,3,2,0:T(8,128)(2,1)} fusion(bf16[256,32,128]{0,2,1:T(8,128)(2,1)} %copy.11, f32[256,32]{0,1:T(8,128)S(1)} %fusion.22, f32[1,32,128,128]{3,2,1,0:T(8,128)} %all-reduce.2.cloned.1.call-done), kind=kOutput, calls=%fused_computation.16 | convolution fusion | flops 272629760 | bytes 6324224 | tf_op jit(solution)/shard_map/bthd,bhde->bthe/dot_general | solution.py:18
  103.2 118.0 %all-gather.2.cloned.1.call-done = bf16[4096,4096]{1,0:T(8,128)(2,1)} async-done(((bf16[256,4096]{1,0:T(8,128)(2,1)}), bf16[4096,4096]{1,0:T(8,128)(2,1)}) %all-gather.2.cloned.1.call-update) | async-done | bytes 33554448 | tf_op jit(solution)/shard_map/all_gather | solution.py:41
  221.1 16.6 %fusion = bf16[1,256,4096]{2,1,0:T(8,128)(2,1)} fusion(bf16[256,4096]{0,1:T(8,128)(2,1)} %bitcast.42, bf16[4096,4096]{1,0:T(8,128)(2,1)} %all-gather.2.cloned.1.call-done), kind=kOutput, calls=%fused_computation.7 | convolution fusion | flops 8590983168 | bytes 37748736 | tf_op jit(solution)/shard_map/btw,wv->btv/dot_general | solution.py:38
  (2 shorter events, 0.0 us)
Async XLA Ops:
  7.4 3.0 %copy-start = (bf16[1,256,32,128]{3,2,1,0:T(8,128)(2,1)S(1)}, bf16[1,256,32,128]{3,2,1,0:T(8,128)(2,1)}, u32[]{:S(2)}) copy-start(bf16[1,256,32,128]{3,2,1,0:T(8,128)(2,1)} %param.6) | copy-start | bytes 6291460
  7.4 91.3 %all-reduce.2.cloned.1.call-start = ((), (), s32[]{:S(2)}) async-start(), calls=%async_computation | async-start | bytes 4194304 | tf_op jit(solution)/shard_map/psum | solution.py:34
  13.4 207.8 %all-gather.2.cloned.1.call-start = ((), (), s32[]{:S(2)}) async-start(), calls=%async_computation.1 | async-start | bytes 35651584 | tf_op jit(solution)/shard_map/all_gather | solution.py:41
Sparse Core Ops, SparseCore 0:
  13.5 85.1 all-reduce.1
Sparse Core Ops, SparseCore 1:
  16.3 204.8 all-gather.1
where the time goes:
time: 246 us; the launch traced here: 245 us
  waiting for transfers between devices  160 us (65%)
  blocking collectives  32.7 us (13%)
  matrix products  26.6 us (11%)
  between operations  14.9 us (6%)
  other arithmetic  6.97 us (3%)
  local copies, waits for them, and re-layouts  4.31 us (2%)
    all_gather x1, waiting for transfers between devices, body(): lax.all_gather(out_weight, 'dp', axis=0, tiled=True)  118 us
    psum x1, waiting for transfers between devices, body(): state, mass = lax.psum((part_state, part_mass), 'sp')  41.1 us
    psum x1, blocking collectives, body(): state, mass = lax.psum((part_state, part_mass), 'sp')  32.7 us
    dot_general x1, matrix products, body(): jnp.einsum('btw,wv->btv', mixed, lax.all_gather(out_weight, 'dp', axis=0,...  16.6 us
  transfers between devices with their start and end apart: 2, of which 2 were waited for; matrix products, arithmetic and copies ran while one was open for 6% of the time, Pallas kernels for 0%

commit v1 on v0

v1 whole, which is shorter than its diff:
```python
import functools

import jax
import jax.numpy as jnp
from jax import lax
from jax.experimental import pallas as pl
from jax.experimental.pallas import tpu as pltpu
from jax.sharding import PartitionSpec as P

MESH = pl.DeviceIdType.MESH
RING = 4
DEPTH = 8
HEADS = 32
SIZE = 128
TOKENS = 256
NEAR = 128
ROWS = TOKENS + 2 * NEAR
BLOCK = 256
WIDTH = 4096
PITCH = 40
WAVES = (512, 512)
STARTS = (0, 1024)
PAIRS = HEADS // 2
SUMS = 2 * SIZE + 8
SENT = 2 * SIZE + 32
F32 = jnp.float32
BF16 = jnp.bfloat16


def feature(values):
    return jnp.where(values > 0.0, values + 1.0, jnp.exp(jnp.minimum(values, 0.0)))


def kernel(
    q_hbm,
    k_hbm,
    v_hbm,
    w_hbm,
    out_hbm,
    w0,
    w1,
    k_in,
    v_in,
    near,
    wide,
    part,
    from_left,
    from_right,
    held,
    mixed,
    acc,
    done0,
    done1,
    local_sem,
    send_sem,
    recv_sem,
):
    dp = lax.axis_index("dp")
    z = lax.axis_index("sp")
    y, x = dp // RING, dp % RING
    half = z % 2
    weights, done = (w0, w1), (done0, done1)

    def z_dev(step):
        return {"sp": (z + step + DEPTH) % DEPTH}

    def flat_dev(along, step):
        if along == "x":
            return {"dp": y * RING + (x + step + RING) % RING}
        return {"dp": ((y + step + RING) % RING) * RING + x}

    ids = {}
    sent = []

    def message(key, src, dst, device):
        i = ids.setdefault(key, len(ids))
        return pltpu.make_async_remote_copy(
            src_ref=src,
            dst_ref=dst,
            send_sem=send_sem.at[i],
            recv_sem=recv_sem.at[i],
            device_id=device,
            device_id_type=MESH,
        )

    def send(key, src, dst, device):
        copy = message(key, src, dst, device)
        copy.start()
        sent.append(copy)

    def receive(key, ref, device):
        message(key, ref, ref, device).wait_recv()

    firsts, seconds = ("x", "y"), ("y", "x")
    f_at, g_at = (x, y), (y, x)

    def block(t, wave, df, dg, rows=None):
        f = (f_at[t] + df + RING) % RING
        g = (g_at[t] + dg + RING) % RING
        start = pl.multiple_of((g * RING + f) * BLOCK, BLOCK)
        if rows is None:
            return weights[wave].at[t, pl.ds(start, BLOCK), :]
        return weights[wave].at[t, pl.ds(pl.multiple_of(start + rows * (BLOCK // 2), BLOCK // 2), BLOCK // 2), :]

    def send_first(t, wave):
        for d in (1, -1):
            ref = block(t, wave, 0, 0)
            send(("first", t, wave, d), ref, ref, flat_dev(firsts[t], d))

    def take_first(t, wave, d):
        receive(("first", t, wave, d), block(t, wave, -d, 0), flat_dev(firsts[t], d))

    def send_first_half(t, wave, d):
        ref = block(t, wave, -d, 0, 0 if d == 1 else 1)
        send(("first half", t, wave, d), ref, ref, flat_dev(firsts[t], d))

    def take_first_half(t, wave, d):
        receive(("first half", t, wave, d), block(t, wave, -2 * d, 0, 0 if d == 1 else 1), flat_dev(firsts[t], d))

    def send_second(t, wave, j):
        for d in (1, -1):
            ref = block(t, wave, j, 0)
            send(("second", t, wave, d, j), ref, ref, flat_dev(seconds[t], d))

    def pass_second(t, wave, j):
        for d in (1, -1):
            receive(("second", t, wave, d, j), block(t, wave, j, -d), flat_dev(seconds[t], d))
            ref = block(t, wave, j, -d, 0 if d == 1 else 1)
            send(("second half", t, wave, d, j), ref, ref, flat_dev(seconds[t], d))

    def take_second_half(t, wave, j):
        for d in (1, -1):
            ref = block(t, wave, j, -2 * d, 0 if d == 1 else 1)
            receive(("second half", t, wave, d, j), ref, flat_dev(seconds[t], d))

    def gather_1(wave):
        for t in (0, 1):
            for d in (1, -1):
                take_first(t, wave, d)
                send_first_half(t, wave, d)
        for j in (-1, 1):
            for t in (0, 1):
                send_second(t, wave, j)

    def gather_2(wave):
        for t in (0, 1):
            for d in (1, -1):
                take_first_half(t, wave, d)
        for t in (0, 1):
            send_second(t, wave, 2)

    def gather_3(wave, j):
        for t in (0, 1):
            pass_second(t, wave, j)

    def gather_4(wave):
        for j in (0, -1, 1, 2):
            for t in (0, 1):
                take_second_half(t, wave, j)

    loads = []
    for wave in (0, 1):
        for t in (0, 1):
            start = pl.multiple_of(half * (WIDTH // 2) + STARTS[wave] + t * WAVES[wave], 128)
            loads.append(
                pltpu.make_async_copy(
                    w_hbm.at[:, pl.ds(start, WAVES[wave])], block(t, wave, 0, 0), local_sem.at[2 * wave + t]
                )
            )
    k_load = pltpu.make_async_copy(k_hbm, k_in, local_sem.at[4])
    v_load = pltpu.make_async_copy(v_hbm, v_in, local_sem.at[5])
    for load in loads:
        load.start()
    k_load.start()
    v_load.start()

    barrier = pltpu.get_barrier_semaphore()
    around = [flat_dev("x", 1), flat_dev("x", -1), flat_dev("y", 1), flat_dev("y", -1), z_dev(1), z_dev(-1)]
    for device in around:
        pl.semaphore_signal(barrier, inc=1, device_id=device, device_id_type=MESH)
    pl.semaphore_wait(barrier, len(around))

    for wave in (0,):
        for t in (0, 1):
            loads[2 * wave + t].wait()
        for t in (0, 1):
            send_first(t, wave)
        for t in (0, 1):
            send_second(t, wave, 0)
    send(("q", 1), q_hbm.at[pl.ds(NEAR * HEADS, NEAR * HEADS), :], near.at[0], z_dev(1))
    send(("q", -1), q_hbm.at[pl.ds(0, NEAR * HEADS), :], near.at[1], z_dev(-1))

    def widen(src, at, count, fn):
        def step(i, carry):
            for u in range(4):
                row = pl.multiple_of((i * 4 + u) * HEADS, HEADS)
                to = pl.multiple_of((at + i * 4 + u) * PITCH, 8)
                wide[pl.ds(to, HEADS), :] = fn(src(row))
            return carry

        lax.fori_loop(0, count // 4, step, 0)

    def as_feature(values):
        return feature(values.astype(F32)).astype(BF16).astype(F32)

    k_load.wait()
    widen(lambda row: k_in[pl.ds(row, HEADS), :], 0, TOKENS, as_feature)
    q_load = pltpu.make_async_copy(q_hbm, k_in, local_sem.at[6])
    q_load.start()
    v_load.wait()
    widen(lambda row: v_in[pl.ds(row, HEADS), :], TOKENS, TOKENS, lambda values: values.astype(F32))

    gather_1(0)

    sub = lax.broadcasted_iota(jnp.int32, (8, SIZE), 0)

    def states(i, carry):
        masses = []
        for u in (0, 1):
            head = 2 * i + u
            keys = wide[pl.ds(head, TOKENS, stride=PITCH), :]
            values = wide[pl.ds(TOKENS * PITCH + head, TOKENS, stride=PITCH), :]
            part[i, pl.ds(u * SIZE, SIZE), :] = lax.dot_general(
                keys.astype(BF16), values.astype(BF16), (((0,), (0,)), ((), ())), preferred_element_type=F32
            )
            masses.append(jnp.sum(keys, axis=0, keepdims=True))
        part[i, pl.ds(2 * SIZE, 8), :] = jnp.where(sub == 0, masses[0], jnp.where(sub == 1, masses[1], 0.0))
        return carry

    lax.fori_loop(0, PAIRS, states, 0)

    def at(chunk, u):
        return ((chunk + 2 * DEPTH) % DEPTH) * 2 + u

    lands = {1: from_left, -1: from_right}

    def reduce_send(d, step, u):
        send(("sum", d, step, u), part.at[at(z + d * (5 - step), u)], lands[d].at[2 * (step - 1) + u], z_dev(d))

    def reduce_add(d, step, u):
        slot = 2 * (step - 1) + u
        receive(("sum", d, step, u), lands[d].at[slot], z_dev(d))
        mine = at(z + d * (4 - step), u)
        part[mine] = part[mine] + lands[d][slot]

    for d, u in ((1, 0), (-1, 1)):
        reduce_send(d, 1, u)
    for d, u in ((1, 1), (-1, 0)):
        reduce_send(d, 2, u)

    for wave in (1,):
        for t in (0, 1):
            loads[2 * wave + t].wait()
        for t in (0, 1):
            send_first(t, wave)
        for t in (0, 1):
            send_second(t, wave, 0)

    q_load.wait()
    widen(lambda row: k_in[pl.ds(row, HEADS), :], 0, TOKENS, as_feature)
    gather_2(0)
    gather_3(0, 0)

    for d, u in ((1, 0), (-1, 1)):
        reduce_add(d, 1, u)
        reduce_send(d, 2, u)

    for slot, (d, first) in enumerate(((1, NEAR), (-1, 0))):
        receive(("q", d), near.at[slot], z_dev(d))
        widen(lambda row, slot=slot: near[slot, pl.ds(row, HEADS), :], TOKENS + slot * NEAR, NEAR, as_feature)
    gather_3(0, -1)

    for u in (1, 0):
        for d in (1, -1):
            v = u if d == 1 else 1 - u
            reduce_add(d, 2, v)
            reduce_send(d, 3, v)
    gather_3(0, 1)
    gather_1(1)

    for u in (1, 0):
        for d in (1, -1):
            v = u if d == 1 else 1 - u
            reduce_add(d, 3, v)
            reduce_send(d, 4, v)
    gather_3(0, 2)

    def gather_send(d, step, u):
        ref = held.at[at(z - d * (step - 1), u)]
        send(("state", d, step, u), ref, ref, z_dev(d))

    def gather_take(d, step, u):
        receive(("state", d, step, u), held.at[at(z - d * step, u)], z_dev(d))

    def read_pair(i):
        terms = held[i, pl.ds(2 * SIZE, 32), :].astype(F32)
        block_at = i
        other_at = (i % RING) * RING + i // RING
        for u in (0, 1):
            head = 2 * i + u
            mass = terms[u : u + 1] + terms[8 + u : 9 + u] + terms[16 + u : 17 + u]
            state = held[i, pl.ds(u * SIZE, SIZE), :]
            for r in range(0, ROWS, 256):
                ask = wide[pl.ds(r * PITCH + head, 256, stride=PITCH), :]
                bottom = jnp.sum(ask * mass, axis=1, keepdims=True) + 0.001
                top = jnp.dot(ask.astype(BF16), state, preferred_element_type=F32)
                result = (top * (2048.0**0.5 / bottom)).astype(BF16)
                for t, b in ((0, block_at), (1, other_at)):
                    to = pl.multiple_of(b * BLOCK + u * SIZE, SIZE)
                    mixed[t, pl.ds(r, 256), pl.ds(to, SIZE)] = result

    def read_chunk(chunk, subs):
        first, count = subs

        def step(j, carry):
            read_pair(at(chunk, 0) + first + j)
            return carry

        lax.fori_loop(0, count, step, 0)

    mine = at(z, 0)
    for u in (0, 1):
        for d in (1, -1):
            receive(("sum", d, 4, u), lands[d].at[6 + u], z_dev(d))
        total = (part[mine + u] + from_left[6 + u] + from_right[6 + u]) * (1.0 / 2048.0)
        held[mine + u, pl.ds(0, 2 * SIZE), :] = total[: 2 * SIZE].astype(BF16)
        mass = total[2 * SIZE :]
        high = mass.astype(BF16).astype(F32)
        middle = (mass - high).astype(BF16).astype(F32)
        low = mass - high - middle
        terms = jnp.concatenate([high, middle, low, jnp.zeros_like(low)], axis=0)
        held[mine + u, pl.ds(2 * SIZE, 32), :] = terms.astype(BF16)
        for d in (1, -1):
            gather_send(d, 1, u)

    read_chunk(z, (0, 2))
    gather_4(0)
    for step in (1, 2, 3):
        for u in (0, 1):
            for d in (1, -1):
                gather_take(d, step, u)
                if step < 3 or (u == 0) == (d == 1):
                    gather_send(d, step + 1, u)
        if step == 2:
            gather_3(1, 0)
        for d in (1, -1):
            read_chunk(z - d * step, (0, 2))
    gather_2(1)
    gather_take(1, 4, 0)
    gather_take(-1, 4, 1)
    read_chunk(z + 4, (0, 2))

    gather_3(1, -1)

    out_at = [half * (WIDTH // 2) + start for start in STARTS]
    own_stores = []

    def finish(wave, rows_at):
        columns = 2 * WAVES[wave]
        start = pl.multiple_of(out_at[wave], 128)
        if rows_at == TOKENS:
            send(
                ("out", wave, -1),
                done[wave].at[pl.ds(TOKENS, NEAR), :],
                out_hbm.at[pl.ds(NEAR, NEAR), pl.ds(start, columns)],
                z_dev(-1),
            )
            send(
                ("out", wave, 1),
                done[wave].at[pl.ds(TOKENS + NEAR, NEAR), :],
                out_hbm.at[pl.ds(0, NEAR), pl.ds(start, columns)],
                z_dev(1),
            )
        else:
            copy = pltpu.make_async_copy(
                done[wave].at[pl.ds(0, TOKENS), :],
                out_hbm.at[pl.ds(0, TOKENS), pl.ds(start, columns)],
                local_sem.at[7 + wave],
            )
            copy.start()
            own_stores.append(copy)

    TILE = 256

    def multiply(wave, rows_at, groups, first, last):
        for t in (0, 1):

            def step(n, carry, t=t):
                column = pl.multiple_of(n * TILE, TILE)
                to = pl.multiple_of(t * WAVES[wave] + n * TILE, TILE)
                rows = pl.ds(rows_at, 256)
                total = None if first else acc[rows, pl.ds(to, TILE)]
                if groups is None:
                    total = jnp.dot(
                        mixed[t, rows, :], weights[wave][t, :, pl.ds(column, TILE)], preferred_element_type=F32
                    )
                else:
                    for dg in groups:
                        g = (g_at[t] + dg + RING) % RING
                        depth = pl.ds(pl.multiple_of(g * RING * BLOCK, RING * BLOCK), RING * BLOCK)
                        product = jnp.dot(
                            mixed[t, rows, depth],
                            weights[wave][t, depth, pl.ds(column, TILE)],
                            preferred_element_type=F32,
                        )
                        total = product if total is None else total + product
                if last:
                    done[wave][rows, pl.ds(to, TILE)] = total.astype(BF16)
                else:
                    acc[rows, pl.ds(to, TILE)] = total
                return carry

            lax.fori_loop(0, WAVES[wave] // TILE, step, 0)

    multiply(0, TOKENS, None, True, True)
    finish(0, TOKENS)
    gather_3(1, 1)
    multiply(0, 0, None, True, True)
    finish(0, 0)
    gather_3(1, 2)
    for rows_at in (TOKENS, 0):
        multiply(1, rows_at, (0, -1, 1), True, False)
    gather_4(1)
    for rows_at in (TOKENS, 0):
        multiply(1, rows_at, (2,), False, True)
        finish(1, rows_at)

    for copy in own_stores:
        copy.wait()
    for copy in sent:
        copy.wait_send()
    for wave in (0, 1):
        columns = 2 * WAVES[wave]
        start = pl.multiple_of((1 - half) * (WIDTH // 2) + STARTS[wave], 128)
        receive(("out", wave, -1), out_hbm.at[pl.ds(NEAR, NEAR), pl.ds(start, columns)], z_dev(-1))
        receive(("out", wave, 1), out_hbm.at[pl.ds(0, NEAR), pl.ds(start, columns)], z_dev(1))
    assert len(ids) <= MESSAGES, len(ids)


MESSAGES = 114


def body(query_rows, key_rows, value_rows, out_weight):
    rows = [a.reshape(TOKENS * HEADS, SIZE) for a in (query_rows, key_rows, value_rows)]
    anywhere = pl.BlockSpec(memory_space=pltpu.HBM)
    result = pl.pallas_call(
        kernel,
        out_shape=jax.ShapeDtypeStruct((TOKENS, WIDTH), BF16),
        in_specs=[anywhere] * 4,
        out_specs=anywhere,
        scratch_shapes=[
            pltpu.VMEM((2, WIDTH, WAVES[0]), BF16),
            pltpu.VMEM((2, WIDTH, WAVES[1]), BF16),
            pltpu.VMEM((TOKENS * HEADS, SIZE), BF16),
            pltpu.VMEM((TOKENS * HEADS, SIZE), BF16),
            pltpu.VMEM((2, NEAR * HEADS, SIZE), BF16),
            pltpu.VMEM((ROWS * PITCH, SIZE), F32),
            pltpu.VMEM((PAIRS, SUMS, SIZE), F32),
            pltpu.VMEM((8, SUMS, SIZE), F32),
            pltpu.VMEM((8, SUMS, SIZE), F32),
            pltpu.VMEM((PAIRS, SENT, SIZE), BF16),
            pltpu.VMEM((2, ROWS, WIDTH), BF16),
            pltpu.VMEM((ROWS, 2 * WAVES[1]), F32),
            pltpu.VMEM((ROWS, 2 * WAVES[0]), BF16),
            pltpu.VMEM((ROWS, 2 * WAVES[1]), BF16),
            pltpu.SemaphoreType.DMA((9,)),
            pltpu.SemaphoreType.DMA((MESSAGES,)),
            pltpu.SemaphoreType.DMA((MESSAGES,)),
        ],
        compiler_params=pltpu.CompilerParams(
            collective_id=0, has_side_effects=True, vmem_limit_bytes=60 * 1024 * 1024
        ),
        name="attend",
    )(*rows, out_weight)
    return result.reshape(1, TOKENS, WIDTH)


def solution(mesh):
    placed = (
        P(("shift", "dp"), "sp", None, None),
        P(("shift", "dp"), "sp", None, None),
        P(("shift", "dp"), "sp", None, None),
        P(("shift", "dp"), None),
    )
    return jax.shard_map(
        body, mesh=mesh, in_specs=placed, out_specs=P(("shift", "dp"), "sp", None), check_vma=False
    )
```

time: 246 us -> 114 us (0.46)
  waiting for transfers between devices: 160 us -> 0 us
  Pallas kernels: 0 us -> 111 us
  blocking collectives: 32.7 us -> 0 us
  matrix products: 26.6 us -> 0 us
  between operations: 14.9 us -> 0.01 us
  other arithmetic: 6.97 us -> 0 us
    all_gather x1 -> x0, waiting for transfers between devices: 118 us -> none  [body(): lax.all_gather(out_weight, 'dp', axis=0, tiled=True)]
    pallas_call x0 -> x1, Pallas kernels: none -> 111 us  [body(): pl.pallas_call(kernel, out_shape=jax.ShapeDtypeStruct((TOKENS, WIDTH), BF...]
    psum x1 -> x0, waiting for transfers between devices: 41.1 us -> none  [body(): state, mass = lax.psum((part_state, part_mass), 'sp')]
    psum x1 -> x0, blocking collectives: 32.7 us -> none  [body(): state, mass = lax.psum((part_state, part_mass), 'sp')]
    dot_general x4 -> x0, matrix products: 26.6 us -> none  [the longest x1 16.6 us: body(): jnp.einsum('btw,wv->btv', mixed, lax.all_gather(out_weight, 'dp', axis=0,...]
    another operation x1 -> x0, local copies, waits for them, and re-layouts: 4.3 us -> none
    another operation x1 -> x0, other arithmetic: 4 us -> none
    unnamed x2 -> x1, local copies, waits for them, and re-layouts: 0.01 us -> 3.13 us
  transfers between devices with their start and end apart: 2 -> 0, of which waited for: 2 -> 0; matrix products, arithmetic and copies ran while one was open for 6% -> 0% of each run, Pallas kernels for 0% -> 0%
where the time goes in v1:
time: 114 us
  Pallas kernels  111 us (97%)
  local copies, waits for them, and re-layouts  3.13 us (3%)
    pallas_call x1, Pallas kernels, body(): pl.pallas_call(kernel, out_shape=jax.ShapeDtypeStruct((TOKENS, WIDTH), BF...  111 us
    unnamed x1, local copies, waits for them, and re-layouts  3.13 us

profile of v1, /device:TPU:2, one launch (start us, length us, event | category | flops | bytes accessed | tf_op | source)
XLA Modules:
  0.0 113.9 jit_solution(2685340253501379321)
XLA Ops:
  0.0 110.8 %attend.1 = bf16[256,4096]{1,0:T(8,128)(2,1)} custom-call(bf16[8192,128]{1,0:T(8,128)(2,1)} %bitcast.5, bf16[8192,128]{1,0:T(8,128)(2,1)} %bitcast.6, bf16[8192,128]{1,0:T(8,128)(2,1)} %bitcast.7, bf16[256,4096]{1,0:T(8,128)(2,1)} %w_hbm.1), custom_call_target="tpu_custom_call" | custom-call | tf_op jit(solution)/shard_map/attend/pallas_call | solution.py:446
  110.8 3.1 %copy.6 = bf16[1,256,4096]{2,1,0:T(8,128)(2,1)} copy(bf16[1,256,4096]{2,1,0:T(8,128)(2,1)} %bitcast.4) | data formatting | bytes 4194304

commit v2 on v1

v2 whole, which is shorter than its diff:
```python
import jax
import jax.numpy as jnp
from jax import lax
from jax.experimental import pallas as pl
from jax.experimental.pallas import tpu as pltpu
from jax.sharding import PartitionSpec as P

MESH = pl.DeviceIdType.MESH
RING = 4
DEPTH = 8
HEADS = 32
SIZE = 128
TOKENS = 256
NEAR = 128
OWN = 2 * NEAR
ROWS = TOKENS + OWN
BLOCK = 256
WIDTH = 4096
PITCH = 40
WAVES = (768, 128, 128)
STARTS = tuple(2 * sum(WAVES[:i]) for i in range(len(WAVES)))
PAIRS = HEADS // 2
SUMS = 2 * SIZE + 8
SENT = 2 * SIZE + 32
F32 = jnp.float32
BF16 = jnp.bfloat16


def feature(values):
    return jnp.where(values > 0.0, values + 1.0, jnp.exp(jnp.minimum(values, 0.0)))


def kernel(q_hbm, k_hbm, v_hbm, w_hbm, out, *scratch):
    weights, scratch = scratch[: len(WAVES)], scratch[len(WAVES) :]
    accs, scratch = scratch[: len(WAVES)], scratch[len(WAVES) :]
    done, scratch = scratch[: len(WAVES)], scratch[len(WAVES) :]
    k_in, v_in, near, wide, part, from_left, from_right, held, mixed, local_sem, send_sem, recv_sem = scratch
    dp = lax.axis_index("dp")
    z = lax.axis_index("sp")
    y, x = dp // RING, dp % RING
    half = z % 2

    def z_dev(step):
        return {"sp": (z + step + DEPTH) % DEPTH}

    def flat_dev(along, step):
        if along == "x":
            return {"dp": y * RING + (x + step + RING) % RING}
        return {"dp": ((y + step + RING) % RING) * RING + x}

    ids = {}
    sent = []

    def message(key, src, dst, device):
        i = ids.setdefault(key, len(ids))
        return pltpu.make_async_remote_copy(
            src_ref=src,
            dst_ref=dst,
            send_sem=send_sem.at[i],
            recv_sem=recv_sem.at[i],
            device_id=device,
            device_id_type=MESH,
        )

    def send(key, src, dst, device):
        copy = message(key, src, dst, device)
        copy.start()
        sent.append(copy)

    def receive(key, ref, device):
        message(key, ref, ref, device).wait_recv()

    firsts, seconds = ("x", "y"), ("y", "x")
    f_at, g_at = (x, y), (y, x)

    def block(t, wave, df, dg, rows=None):
        f = (f_at[t] + df + RING) % RING
        g = (g_at[t] + dg + RING) % RING
        start = pl.multiple_of((g * RING + f) * BLOCK, BLOCK)
        if rows is None:
            return weights[wave].at[t, pl.ds(start, BLOCK), :]
        return weights[wave].at[t, pl.ds(pl.multiple_of(start + rows * (BLOCK // 2), BLOCK // 2), BLOCK // 2), :]

    def send_first(t, wave):
        for d in (1, -1):
            ref = block(t, wave, 0, 0)
            send(("first", t, wave, d), ref, ref, flat_dev(firsts[t], d))

    def take_first(t, wave, d):
        receive(("first", t, wave, d), block(t, wave, -d, 0), flat_dev(firsts[t], d))

    def send_first_half(t, wave, d):
        ref = block(t, wave, -d, 0, 0 if d == 1 else 1)
        send(("first half", t, wave, d), ref, ref, flat_dev(firsts[t], d))

    def take_first_half(t, wave, d):
        receive(("first half", t, wave, d), block(t, wave, -2 * d, 0, 0 if d == 1 else 1), flat_dev(firsts[t], d))

    def send_second(t, wave, j):
        for d in (1, -1):
            ref = block(t, wave, j, 0)
            send(("second", t, wave, d, j), ref, ref, flat_dev(seconds[t], d))

    def pass_second(t, wave, j):
        for d in (1, -1):
            receive(("second", t, wave, d, j), block(t, wave, j, -d), flat_dev(seconds[t], d))
            ref = block(t, wave, j, -d, 0 if d == 1 else 1)
            send(("second half", t, wave, d, j), ref, ref, flat_dev(seconds[t], d))

    def take_second_half(t, wave, j):
        for d in (1, -1):
            ref = block(t, wave, j, -2 * d, 0 if d == 1 else 1)
            receive(("second half", t, wave, d, j), ref, flat_dev(seconds[t], d))

    def gather_1(wave):
        for t in (0, 1):
            for d in (1, -1):
                take_first(t, wave, d)
                send_first_half(t, wave, d)
        for j in (-1, 1):
            for t in (0, 1):
                send_second(t, wave, j)

    def gather_2(wave):
        for t in (0, 1):
            for d in (1, -1):
                take_first_half(t, wave, d)
        for t in (0, 1):
            send_second(t, wave, 2)

    def gather_3(wave, j):
        for t in (0, 1):
            pass_second(t, wave, j)

    def gather_4(wave):
        for j in (0, -1, 1, 2):
            for t in (0, 1):
                take_second_half(t, wave, j)

    barrier = pltpu.get_barrier_semaphore()
    around = [flat_dev("x", 1), flat_dev("x", -1), flat_dev("y", 1), flat_dev("y", -1), z_dev(1), z_dev(-1)]
    for device in around:
        pl.semaphore_signal(barrier, inc=1, device_id=device, device_id_type=MESH)
    loads = []
    for wave in range(len(WAVES)):
        for t in (0, 1):
            start = pl.multiple_of(half * (WIDTH // 2) + STARTS[wave] + t * WAVES[wave], 128)
            loads.append(
                pltpu.make_async_copy(
                    w_hbm.at[:, pl.ds(start, WAVES[wave])], block(t, wave, 0, 0), local_sem.at[2 * wave + t]
                )
            )
    k_load = pltpu.make_async_copy(k_hbm, k_in, local_sem.at[2 * len(WAVES)])
    v_load = pltpu.make_async_copy(v_hbm, v_in, local_sem.at[2 * len(WAVES) + 1])
    q_load = pltpu.make_async_copy(q_hbm, k_in, local_sem.at[2 * len(WAVES) + 2])
    for load in loads[:2] + [k_load, v_load] + loads[2:]:
        load.start()
    pl.semaphore_wait(barrier, len(around))

    def send_own(wave):
        for t in (0, 1):
            loads[2 * wave + t].wait()
        for t in (0, 1):
            send_first(t, wave)
        for t in (0, 1):
            send_second(t, wave, 0)

    QUARTER = NEAR // 2

    def near_rows(d, late):
        row = (0 if d == 1 else NEAR) + (QUARTER if late == (d == -1) else 0)
        return near.at[pl.ds(row * HEADS, QUARTER * HEADS), :], row

    def send_queries(late):
        for d in (1, -1):
            position = {(1, True): NEAR, (1, False): NEAR + QUARTER, (-1, False): 0, (-1, True): QUARTER}[d, late]
            ref, _ = near_rows(d, late)
            send(("q", d, late), q_hbm.at[pl.ds(position * HEADS, QUARTER * HEADS), :], ref, z_dev(d))

    send_own(0)
    send_queries(False)

    def widen(src, at, count, fn):
        def step(i, carry):
            for u in range(4):
                row = pl.multiple_of((i * 4 + u) * HEADS, HEADS)
                to = pl.multiple_of((at + i * 4 + u) * PITCH, 8)
                wide[pl.ds(to, HEADS), :] = fn(src(row))
            return carry

        lax.fori_loop(0, count // 4, step, 0)

    def as_feature(values):
        return feature(values.astype(F32)).astype(BF16).astype(F32)

    k_load.wait()
    widen(lambda row: k_in[pl.ds(row, HEADS), :], 0, TOKENS, as_feature)
    q_load.start()
    v_load.wait()
    widen(lambda row: v_in[pl.ds(row, HEADS), :], TOKENS, TOKENS, lambda values: values.astype(F32))

    sub = lax.broadcasted_iota(jnp.int32, (8, SIZE), 0)

    def states(i, carry):
        masses = []
        for u in (0, 1):
            head = 2 * i + u
            keys = wide[pl.ds(head, TOKENS, stride=PITCH), :]
            values = wide[pl.ds(TOKENS * PITCH + head, TOKENS, stride=PITCH), :]
            part[i, pl.ds(u * SIZE, SIZE), :] = lax.dot_general(
                keys.astype(BF16), values.astype(BF16), (((0,), (0,)), ((), ())), preferred_element_type=F32
            )
            masses.append(jnp.sum(keys, axis=0, keepdims=True))
        part[i, pl.ds(2 * SIZE, 8), :] = jnp.where(sub == 0, masses[0], jnp.where(sub == 1, masses[1], 0.0))
        return carry

    lax.fori_loop(0, PAIRS, states, 0)

    def at(chunk, u):
        return ((chunk + 2 * DEPTH) % DEPTH) * 2 + u

    lands = {1: from_left, -1: from_right}

    def reduce_send(d, step, u):
        send(("sum", d, step, u), part.at[at(z + d * (5 - step), u)], lands[d].at[2 * (step - 1) + u], z_dev(d))

    def reduce_add(d, step, u):
        slot = 2 * (step - 1) + u
        receive(("sum", d, step, u), lands[d].at[slot], z_dev(d))
        mine = at(z + d * (4 - step), u)
        part[mine] = part[mine] + lands[d][slot]

    def widen_queries(late):
        for d in (1, -1):
            ref, row = near_rows(d, late)
            receive(("q", d, late), ref, z_dev(d))
            widen(lambda at, row=row: near[pl.ds(row * HEADS + at, HEADS), :], row, QUARTER, as_feature)

    for d, u in ((1, 0), (-1, 1)):
        reduce_send(d, 1, u)
    for d, u in ((1, 1), (-1, 0)):
        reduce_send(d, 2, u)
    gather_1(0)
    for wave in (1, 2):
        send_own(wave)

    q_load.wait()
    widen(lambda row: k_in[pl.ds(row, HEADS), :], OWN, TOKENS, as_feature)
    widen_queries(False)

    for d, u in ((1, 0), (-1, 1)):
        reduce_add(d, 1, u)
        reduce_send(d, 2, u)
    gather_3(0, 0)
    for step in (2, 3):
        for u in (1, 0):
            for d in (1, -1):
                v = u if d == 1 else 1 - u
                reduce_add(d, step, v)
                reduce_send(d, step + 1, v)
        if step == 2:
            gather_2(0)
        else:
            gather_3(0, -1)

    def gather_send(d, step, u):
        ref = held.at[at(z - d * (step - 1), u)]
        send(("state", d, step, u), ref, ref, z_dev(d))

    def gather_take(d, step, u):
        receive(("state", d, step, u), held.at[at(z - d * step, u)], z_dev(d))

    def read_pair(i, blocks):
        terms = held[i, pl.ds(2 * SIZE, 32), :].astype(F32)
        block_at = i
        other_at = (i % RING) * RING + i // RING
        for u in (0, 1):
            head = 2 * i + u
            mass = terms[u : u + 1] + terms[8 + u : 9 + u] + terms[16 + u : 17 + u]
            state = held[i, pl.ds(u * SIZE, SIZE), :]
            for r, count in blocks:
                ask = wide[pl.ds(r * PITCH + head, count, stride=PITCH), :]
                bottom = jnp.sum(ask * mass, axis=1, keepdims=True) + 0.001
                top = jnp.dot(ask.astype(BF16), state, preferred_element_type=F32)
                result = (top * (2048.0**0.5 / bottom)).astype(BF16)
                for t, b in ((0, block_at), (1, other_at)):
                    to = pl.multiple_of(b * BLOCK + u * SIZE, SIZE)
                    mixed[t, pl.ds(r, count), pl.ds(to, SIZE)] = result

    EARLY = ((QUARTER, NEAR), (OWN, TOKENS))
    LATE = ((0, QUARTER), (3 * QUARTER, QUARTER))

    def read_pairs(first, count, blocks):
        def step(j, carry):
            read_pair(first + j, blocks)
            return carry

        lax.fori_loop(0, count, step, 0)

    def read_chunk(chunk):
        read_pairs(at(chunk, 0), 2, EARLY)

    mine = at(z, 0)
    for u in (0, 1):
        for d in (1, -1):
            receive(("sum", d, 4, u), lands[d].at[6 + u], z_dev(d))
        total = (part[mine + u] + from_left[6 + u] + from_right[6 + u]) * (1.0 / 2048.0)
        held[mine + u, pl.ds(0, 2 * SIZE), :] = total[: 2 * SIZE].astype(BF16)
        mass = total[2 * SIZE :]
        high = mass.astype(BF16).astype(F32)
        middle = (mass - high).astype(BF16).astype(F32)
        low = mass - high - middle
        terms = jnp.concatenate([high, middle, low, jnp.zeros_like(low)], axis=0)
        held[mine + u, pl.ds(2 * SIZE, 32), :] = terms.astype(BF16)
        for d in (1, -1):
            gather_send(d, 1, u)

    gather_3(0, 1)
    read_chunk(z)
    for step in (1, 2, 3):
        for u in (0, 1):
            for d in (1, -1):
                gather_take(d, step, u)
                if step < 3 or (u == 0) == (d == 1):
                    gather_send(d, step + 1, u)
        if step == 1:
            for wave in (1, 2):
                gather_1(wave)
        if step == 3:
            send_queries(True)
        for d in (1, -1):
            read_chunk(z - d * step)
    gather_take(1, 4, 0)
    gather_take(-1, 4, 1)
    read_chunk(z + 4)
    for wave in (1, 2):
        gather_3(wave, 0)
    gather_3(0, 2)
    widen_queries(True)
    read_pairs(0, PAIRS, LATE)

    def finish(wave):
        columns = pl.ds(pl.multiple_of(half * (WIDTH // 2) + STARTS[wave], 128), 2 * WAVES[wave])
        for d, row, to in ((-1, 0, NEAR), (1, NEAR, 0)):
            send(("out", wave, d), done[wave].at[pl.ds(row, NEAR), :], out.at[pl.ds(to, NEAR), columns], z_dev(d))

    def multiply(wave, rows_at, groups, first, last):
        tile = min(256, WAVES[wave])
        for t in (0, 1):

            def step(n, carry, t=t):
                column = pl.multiple_of(n * tile, tile)
                to = pl.multiple_of(t * WAVES[wave] + n * tile, tile)
                rows = pl.ds(rows_at, 256)
                total = None if first else accs[wave][rows, pl.ds(to, tile)]
                for dg in groups:
                    g = (g_at[t] + dg + RING) % RING
                    depth = pl.ds(pl.multiple_of(g * RING * BLOCK, RING * BLOCK), RING * BLOCK)
                    product = jnp.dot(
                        mixed[t, rows, depth], weights[wave][t, depth, pl.ds(column, tile)], preferred_element_type=F32
                    )
                    total = product if total is None else total + product
                if not last:
                    accs[wave][rows, pl.ds(to, tile)] = total
                elif rows_at == 0:
                    done[wave][:, pl.ds(to, tile)] = total.astype(BF16)
                else:
                    at = pl.multiple_of(half * (WIDTH // 2) + STARTS[wave] + to, 128)
                    out[:, pl.ds(at, tile)] = total.astype(BF16)
                return carry

            lax.fori_loop(0, WAVES[wave] // tile, step, 0)

    for rows_at in (0, OWN):
        multiply(0, rows_at, (0, -1, 1), True, False)
    for wave in (1, 2):
        gather_2(wave)
    gather_4(0)
    multiply(0, 0, (2,), False, True)
    finish(0)
    for wave in (1, 2):
        for j in (-1, 1):
            gather_3(wave, j)
    multiply(0, OWN, (2,), False, True)
    for wave in (1, 2):
        gather_3(wave, 2)
    for wave in (1, 2):
        for rows_at in (0, OWN):
            multiply(wave, rows_at, (0, -1, 1), True, False)
    for wave in (1, 2):
        gather_4(wave)
        multiply(wave, 0, (2,), False, True)
        finish(wave)
        multiply(wave, OWN, (2,), False, True)

    for copy in sent:
        copy.wait_send()
    for wave in range(len(WAVES)):
        columns = pl.ds(pl.multiple_of((1 - half) * (WIDTH // 2) + STARTS[wave], 128), 2 * WAVES[wave])
        for d, to in ((-1, NEAR), (1, 0)):
            receive(("out", wave, d), out.at[pl.ds(to, NEAR), columns], z_dev(d))
    assert len(ids) <= MESSAGES, len(ids)


MESSAGES = 158


def body(query_rows, key_rows, value_rows, out_weight):
    rows = [a.reshape(TOKENS * HEADS, SIZE) for a in (query_rows, key_rows, value_rows)]
    anywhere = pl.BlockSpec(memory_space=pltpu.HBM)
    result = pl.pallas_call(
        kernel,
        out_shape=pltpu.VMEM((TOKENS, WIDTH), BF16),
        in_specs=[anywhere] * 4,
        out_specs=pl.BlockSpec(memory_space=pltpu.VMEM),
        scratch_shapes=[pltpu.VMEM((2, WIDTH, columns), BF16) for columns in WAVES]
        + [pltpu.VMEM((ROWS, 2 * columns), F32) for columns in WAVES]
        + [pltpu.VMEM((OWN, 2 * columns), BF16) for columns in WAVES]
        + [
            pltpu.VMEM((TOKENS * HEADS, SIZE), BF16),
            pltpu.VMEM((TOKENS * HEADS, SIZE), BF16),
            pltpu.VMEM((OWN * HEADS, SIZE), BF16),
            pltpu.VMEM((ROWS * PITCH, SIZE), F32),
            pltpu.VMEM((PAIRS, SUMS, SIZE), F32),
            pltpu.VMEM((8, SUMS, SIZE), F32),
            pltpu.VMEM((8, SUMS, SIZE), F32),
            pltpu.VMEM((PAIRS, SENT, SIZE), BF16),
            pltpu.VMEM((2, ROWS, WIDTH), BF16),
            pltpu.SemaphoreType.DMA((2 * len(WAVES) + 3,)),
            pltpu.SemaphoreType.DMA((MESSAGES,)),
            pltpu.SemaphoreType.DMA((MESSAGES,)),
        ],
        compiler_params=pltpu.CompilerParams(
            collective_id=0, has_side_effects=True, vmem_limit_bytes=56 * 1024 * 1024
        ),
        name="attend",
    )(*rows, out_weight)
    return result.reshape(1, TOKENS, WIDTH)


def solution(mesh):
    placed = (
        P(("shift", "dp"), "sp", None, None),
        P(("shift", "dp"), "sp", None, None),
        P(("shift", "dp"), "sp", None, None),
        P(("shift", "dp"), None),
    )
    return jax.shard_map(
        body, mesh=mesh, in_specs=placed, out_specs=P(("shift", "dp"), "sp", None), check_vma=False
    )
```

time: 114 us -> 105 us (0.921)
  Pallas kernels: 111 us -> 104 us
  local copies, waits for them, and re-layouts: 3.13 us -> 1.32 us
    pallas_call x1, Pallas kernels: 111 us -> 104 us  [body(): pl.pallas_call(kernel, out_shape=pltpu.VMEM((TOKENS, WIDTH), BF16), in_sp...]
    unnamed x1, local copies, waits for them, and re-layouts: 3.13 us -> 1.32 us
where the time goes in v2:
time: 105 us
  Pallas kernels  104 us (99%)
  local copies, waits for them, and re-layouts  1.32 us (1%)
    pallas_call x1, Pallas kernels, body(): pl.pallas_call(kernel, out_shape=pltpu.VMEM((TOKENS, WIDTH), BF16), in_sp...  104 us

profile of v2, /device:TPU:2, one launch (start us, length us, event | category | flops | bytes accessed | tf_op | source)
XLA Modules:
  0.0 105.2 jit_solution(15619048518329196481)
XLA Ops:
  0.0 103.8 %attend.1 = bf16[256,4096]{1,0:T(8,128)(2,1)S(1)} custom-call(bf16[8192,128]{1,0:T(8,128)(2,1)} %bitcast.5, bf16[8192,128]{1,0:T(8,128)(2,1)} %bitcast.6, bf16[8192,128]{1,0:T(8,128)(2,1)} %bitcast.7, bf16[256,4096]{1,0:T(8,128)(2,1)} %w_hbm.1), custom_call_target="tpu_custom_call" | custom-call | tf_op jit(solution)/shard_map/attend/pallas_call | solution.py:411
  103.9 1.3 %copy.6 = bf16[1,256,4096]{2,1,0:T(8,128)(2,1)} copy(bf16[1,256,4096]{2,1,0:T(8,128)(2,1)S(1)} %bitcast.4) | data formatting | bytes 4194304

commit v3 on v2

v3 whole, which is shorter than its diff:
```python
import jax
import jax.numpy as jnp
from jax import lax
from jax.experimental import pallas as pl
from jax.experimental.pallas import tpu as pltpu
from jax.sharding import PartitionSpec as P

MESH = pl.DeviceIdType.MESH
RING = 4
DEPTH = 8
HEADS = 32
SIZE = 128
TOKENS = 256
NEAR = 128
OWN = 2 * NEAR
ROWS = TOKENS + OWN
BLOCK = 256
WIDTH = 4096
PITCH = 40
WAVES = (512, 128, 128, 128, 128)
GIVE, TAKE = 1, 2
PAIRS = HEADS // 2
SUMS = 2 * SIZE + 8
SENT = 2 * SIZE + 32
F32 = jnp.float32
BF16 = jnp.bfloat16


def feature(values):
    return jnp.where(values > 0.0, values + 1.0, jnp.exp(jnp.minimum(values, 0.0)))


def kernel(q_hbm, k_hbm, v_hbm, w_hbm, out, *scratch):
    weights, scratch = scratch[: len(WAVES)], scratch[len(WAVES) :]
    acc, scratch = scratch[0], scratch[1:]
    done, scratch = scratch[: len(WAVES)], scratch[len(WAVES) :]
    k_in, v_in, near, wide, part, from_left, from_right, held, mixed, local_sem, send_sem, recv_sem = scratch
    dp = lax.axis_index("dp")
    z = lax.axis_index("sp")
    y, x = dp // RING, dp % RING
    half = z % 2

    def z_dev(step):
        return {"sp": (z + step + DEPTH) % DEPTH}

    def flat_dev(along, step):
        if along == "x":
            return {"dp": y * RING + (x + step + RING) % RING}
        return {"dp": ((y + step + RING) % RING) * RING + x}

    turn = (z // 2) % 2

    def columns_at(wave):
        start = 2 * sum(WAVES[:wave])
        if wave == GIVE:
            return start + 2 * WAVES[GIVE] * turn
        if wave == TAKE:
            return start - 2 * WAVES[GIVE] * turn
        return start

    send_ids, ids = {}, {}

    def copy_of(sent, key, src, dst, device):
        return pltpu.make_async_remote_copy(
            src_ref=src,
            dst_ref=dst,
            send_sem=send_sem.at[send_ids.setdefault(sent, len(send_ids))],
            recv_sem=recv_sem.at[ids.setdefault(key, len(ids))],
            device_id=device,
            device_id_type=MESH,
        )

    def send(sent, key, src, dst, device):
        copy_of(sent, key, src, dst, device).start()

    def receive(key, ref):
        copy_of(("own", 0), key, ref, ref, z_dev(1)).wait_recv()

    def all_sent(sent, ref):
        copy_of(sent, ("first", 0), ref, ref, z_dev(1)).wait_send()

    firsts, seconds = ("x", "y"), ("y", "x")
    f_at, g_at = (x, y), (y, x)

    def block(t, wave, df, dg, rows=None):
        f = (f_at[t] + df + RING) % RING
        g = (g_at[t] + dg + RING) % RING
        start = pl.multiple_of((g * RING + f) * BLOCK, BLOCK)
        if rows is None:
            return weights[wave].at[t, pl.ds(start, BLOCK), :]
        return weights[wave].at[t, pl.ds(pl.multiple_of(start + rows * (BLOCK // 2), BLOCK // 2), BLOCK // 2), :]

    def both(wave, blocks):
        return weights[wave].at[:, pl.ds(0, blocks * BLOCK), :]

    def pass_on(what, t, wave, ref, along, d):
        send(("own", wave), (what, wave), ref, ref, flat_dev(along[t], d))

    def send_second(t, wave, j):
        for d in (1, -1):
            pass_on(("second", j), t, wave, block(t, wave, j, 0), seconds, d)

    def gather_1(wave):
        receive(("first", wave), both(wave, 2))
        for t in (0, 1):
            for d in (1, -1):
                pass_on("first half", t, wave, block(t, wave, -d, 0, 0 if d == 1 else 1), firsts, d)
        for j in (-1, 1):
            for t in (0, 1):
                send_second(t, wave, j)

    def gather_2(wave):
        receive(("first half", wave), both(wave, 1))
        for t in (0, 1):
            send_second(t, wave, 2)

    def gather_3(wave, j):
        receive((("second", j), wave), both(wave, 2))
        if wave != TAKE:
            for t in (0, 1):
                for d in (1, -1):
                    pass_on("second half", t, wave, block(t, wave, j, -d, 0 if d == 1 else 1), seconds, d)

    def relay():
        for t in (0, 1):
            for d in (1, -1):
                g = (g_at[t] + 2) % RING
                rows = pl.ds(pl.multiple_of((g * RING + (0 if d == 1 else 2)) * BLOCK, BLOCK), 2 * BLOCK)
                send(
                    "relay",
                    ("second half", TAKE),
                    weights[GIVE].at[t, rows, :],
                    weights[TAKE].at[t, rows, :],
                    z_dev(2 * d),
                )

    def gather_4(wave):
        receive(("second half", wave), both(wave, 4))

    barrier = pltpu.get_barrier_semaphore()
    around = [flat_dev("x", 1), flat_dev("x", -1), flat_dev("y", 1), flat_dev("y", -1), z_dev(1), z_dev(-1)]
    around += [z_dev(2), z_dev(-2)]
    for device in around:
        pl.semaphore_signal(barrier, inc=1, device_id=device, device_id_type=MESH)
    loads = []
    for wave in range(len(WAVES)):
        for t in (0, 1):
            start = pl.multiple_of(half * (WIDTH // 2) + columns_at(wave) + t * WAVES[wave], 128)
            loads.append(
                pltpu.make_async_copy(
                    w_hbm.at[:, pl.ds(start, WAVES[wave])], block(t, wave, 0, 0), local_sem.at[wave]
                )
            )
    k_load = pltpu.make_async_copy(k_hbm, k_in, local_sem.at[len(WAVES)])
    v_load = pltpu.make_async_copy(v_hbm, v_in, local_sem.at[len(WAVES) + 1])
    q_load = pltpu.make_async_copy(q_hbm, k_in, local_sem.at[len(WAVES) + 2])
    for load in loads[:2] + [k_load, v_load] + loads[2:]:
        load.start()
    pl.semaphore_wait(barrier, len(around))

    def send_own(wave):
        ref = both(wave, 1)
        pltpu.make_async_copy(ref, ref, local_sem.at[wave]).wait()
        for t in (0, 1):
            for d in (1, -1):
                pass_on("first", t, wave, block(t, wave, 0, 0), firsts, d)
        for t in (0, 1):
            send_second(t, wave, 0)

    LOTS = ((0, 32), (32, 32), (64, 64))
    SOON = LOTS[0][1]

    def near_row(d, lot):
        start, count = LOTS[lot]
        return NEAR - start - count if d == 1 else NEAR + start

    def near_rows(d, lot):
        return near.at[pl.ds(near_row(d, lot) * HEADS, LOTS[lot][1] * HEADS), :]

    def send_queries(lot):
        for d in (1, -1):
            start, count = LOTS[lot]
            position = TOKENS - start - count if d == 1 else start
            send(
                "q",
                ("q", lot),
                q_hbm.at[pl.ds(position * HEADS, count * HEADS), :],
                near_rows(d, lot),
                z_dev(d),
            )

    send_own(0)
    send_own(GIVE)
    send_queries(0)

    def widen(src, at, count, fn):
        def step(i, carry):
            for u in range(4):
                row = pl.multiple_of((i * 4 + u) * HEADS, HEADS)
                to = pl.multiple_of((at + i * 4 + u) * PITCH, 8)
                wide[pl.ds(to, HEADS), :] = fn(src(row))
            return carry

        lax.fori_loop(0, count // 4, step, 0)

    def as_feature(values):
        return feature(values.astype(F32)).astype(BF16).astype(F32)

    k_load.wait()
    widen(lambda row: k_in[pl.ds(row, HEADS), :], 0, TOKENS, as_feature)
    q_load.start()
    v_load.wait()
    widen(lambda row: v_in[pl.ds(row, HEADS), :], TOKENS, TOKENS, lambda values: values.astype(F32))

    sub = lax.broadcasted_iota(jnp.int32, (8, SIZE), 0)

    def states(i, carry):
        masses = []
        for u in (0, 1):
            head = 2 * i + u
            keys = wide[pl.ds(head, TOKENS, stride=PITCH), :]
            values = wide[pl.ds(TOKENS * PITCH + head, TOKENS, stride=PITCH), :]
            part[i, pl.ds(u * SIZE, SIZE), :] = lax.dot_general(
                keys.astype(BF16), values.astype(BF16), (((0,), (0,)), ((), ())), preferred_element_type=F32
            )
            masses.append(jnp.sum(keys, axis=0, keepdims=True))
        part[i, pl.ds(2 * SIZE, 8), :] = jnp.where(sub == 0, masses[0], jnp.where(sub == 1, masses[1], 0.0))
        return carry

    lax.fori_loop(0, PAIRS, states, 0)

    def at(chunk, u):
        return ((chunk + 2 * DEPTH) % DEPTH) * 2 + u

    lands = {1: from_left, -1: from_right}

    def reduce_send(d, step, u):
        send("sum", ("sum", d, step, u), part.at[at(z + d * (5 - step), u)], lands[d].at[2 * (step - 1) + u], z_dev(d))

    def reduce_add(d, step, u):
        slot = 2 * (step - 1) + u
        receive(("sum", d, step, u), lands[d].at[slot])
        mine = at(z + d * (4 - step), u)
        part[mine] = part[mine] + lands[d][slot]

    def widen_queries(lot):
        receive(("q", lot), near.at[pl.ds(0, 2 * LOTS[lot][1] * HEADS), :])
        for d in (1, -1):
            row = near_row(d, lot)
            widen(lambda at, row=row: near[pl.ds(row * HEADS + at, HEADS), :], row, LOTS[lot][1], as_feature)

    for d, u in ((1, 0), (-1, 1)):
        reduce_send(d, 1, u)
    for d, u in ((1, 1), (-1, 0)):
        reduce_send(d, 2, u)
    gather_1(0)

    q_load.wait()
    widen(lambda row: k_in[pl.ds(row, HEADS), :], OWN, TOKENS, as_feature)
    widen_queries(0)

    for d, u in ((1, 0), (-1, 1)):
        reduce_add(d, 1, u)
        reduce_send(d, 2, u)
    gather_3(0, 0)
    for step in (2, 3):
        for u in (1, 0):
            for d in (1, -1):
                v = u if d == 1 else 1 - u
                reduce_add(d, step, v)
                reduce_send(d, step + 1, v)
        if step == 2:
            gather_2(0)
            gather_1(1)
        else:
            send_queries(1)
            gather_3(0, -1)
            gather_3(1, 0)

    def gather_send(d, step, u):
        ref = held.at[at(z - d * (step - 1), u)]
        send("state", ("state", d, step, u), ref, ref, z_dev(d))

    def gather_take(d, step, u):
        receive(("state", d, step, u), held.at[at(z - d * step, u)])

    def read_pair(i, blocks):
        terms = held[i, pl.ds(2 * SIZE, 32), :].astype(F32)
        block_at = i
        other_at = (i % RING) * RING + i // RING
        for u in (0, 1):
            head = 2 * i + u
            mass = terms[u : u + 1] + terms[8 + u : 9 + u] + terms[16 + u : 17 + u]
            state = held[i, pl.ds(u * SIZE, SIZE), :]
            for r, count in blocks:
                ask = wide[pl.ds(r * PITCH + head, count, stride=PITCH), :]
                bottom = jnp.sum(ask * mass, axis=1, keepdims=True) + 0.001
                top = jnp.dot(ask.astype(BF16), state, preferred_element_type=F32)
                result = (top * (2048.0**0.5 / bottom)).astype(BF16)
                for t, b in ((0, block_at), (1, other_at)):
                    to = pl.multiple_of(b * BLOCK + u * SIZE, SIZE)
                    mixed[t, pl.ds(r, count), pl.ds(to, SIZE)] = result

    EARLY = ((NEAR - SOON, 2 * SOON), (OWN, TOKENS))
    LATE = ((0, NEAR - SOON), (NEAR + SOON, NEAR - SOON))

    def read_pairs(first, count, blocks):
        def step(j, carry):
            read_pair(first + j, blocks)
            return carry

        lax.fori_loop(0, count, step, 0)

    def read_chunk(chunk):
        read_pairs(at(chunk, 0), 2, EARLY)

    mine = at(z, 0)
    for u in (0, 1):
        for d in (1, -1):
            receive(("sum", d, 4, u), lands[d].at[6 + u])
        total = (part[mine + u] + from_left[6 + u] + from_right[6 + u]) * (1.0 / 2048.0)
        held[mine + u, pl.ds(0, 2 * SIZE), :] = total[: 2 * SIZE].astype(BF16)
        mass = total[2 * SIZE :]
        high = mass.astype(BF16).astype(F32)
        middle = (mass - high).astype(BF16).astype(F32)
        low = mass - high - middle
        terms = jnp.concatenate([high, middle, low, jnp.zeros_like(low)], axis=0)
        held[mine + u, pl.ds(2 * SIZE, 32), :] = terms.astype(BF16)
        for d in (1, -1):
            gather_send(d, 1, u)

    read_chunk(z)
    gather_3(0, 1)
    for step in (1, 2, 3):
        for u in (0, 1):
            for d in (1, -1):
                gather_take(d, step, u)
                if step < 3 or (u == 0) == (d == 1):
                    gather_send(d, step + 1, u)
        if step == 2:
            gather_2(1)
            gather_3(0, 2)
            send_own(2)
        if step == 3:
            send_queries(2)
            gather_3(1, -1)
            gather_3(1, 1)
        for d in (1, -1):
            read_chunk(z - d * step)
    gather_take(1, 4, 0)
    gather_take(-1, 4, 1)
    read_chunk(z + 4)

    def finish(wave):
        columns = pl.ds(pl.multiple_of(half * (WIDTH // 2) + columns_at(wave), 128), 2 * WAVES[wave])
        for d, row, to in ((-1, 0, NEAR), (1, NEAR, 0)):
            send(
                ("out", wave),
                ("out", wave),
                done[wave].at[pl.ds(row, NEAR), :],
                out.at[pl.ds(to, NEAR), columns],
                z_dev(d),
            )

    def multiply(wave, rows_at, groups, first, last):
        tile = 256 if WAVES[wave] % 256 == 0 else 128
        for t in (0, 1):

            def step(n, carry, t=t):
                column = pl.multiple_of(n * tile, tile)
                to = pl.multiple_of(t * WAVES[wave] + n * tile, tile)
                rows = pl.ds(rows_at, 256)
                total = None if first else acc[rows, pl.ds(to, tile)]
                for dg in groups:
                    g = (g_at[t] + dg + RING) % RING
                    depth = pl.ds(pl.multiple_of(g * RING * BLOCK, RING * BLOCK), RING * BLOCK)
                    product = jnp.dot(
                        mixed[t, rows, depth], weights[wave][t, depth, pl.ds(column, tile)], preferred_element_type=F32
                    )
                    total = product if total is None else total + product
                if not last:
                    acc[rows, pl.ds(to, tile)] = total
                elif rows_at == 0:
                    done[wave][:, pl.ds(to, tile)] = total.astype(BF16)
                else:
                    at = pl.multiple_of(half * (WIDTH // 2) + columns_at(wave) + to, 128)
                    out[:, pl.ds(at, tile)] = total.astype(BF16)
                return carry

            lax.fori_loop(0, WAVES[wave] // tile, step, 0)

    WHOLE = (0, -1, 1, 2)

    def near_products(wave):
        multiply(wave, 0, WHOLE, True, True)
        finish(wave)

    def own_products(wave):
        multiply(wave, OWN, WHOLE, True, True)

    send_own(3)
    gather_3(1, 2)
    gather_4(0)
    own_products(0)
    gather_1(2)
    gather_4(1)
    relay()
    send_own(4)
    widen_queries(1)
    widen_queries(2)
    read_pairs(0, PAIRS, LATE)
    gather_3(2, 0)
    gather_1(3)
    gather_2(2)
    near_products(0)
    gather_3(3, 0)
    gather_2(3)
    gather_1(4)
    near_products(1)
    gather_3(2, -1)
    gather_3(2, 1)
    gather_3(3, -1)
    gather_3(3, 1)
    own_products(1)
    gather_3(3, 2)
    gather_3(4, 0)
    gather_2(4)
    gather_3(2, 2)
    gather_4(2)
    near_products(2)
    gather_3(4, -1)
    gather_3(4, 1)
    own_products(2)
    gather_4(3)
    near_products(3)
    gather_3(4, 2)
    own_products(3)
    for rows_at in (0, OWN):
        multiply(4, rows_at, (0, -1, 1), True, False)
    gather_4(4)
    multiply(4, 0, (2,), False, True)
    finish(4)
    multiply(4, OWN, (2,), False, True)

    for wave in range(len(WAVES)):
        all_sent(("own", wave), both(wave, 11 if wave == TAKE else 15))
    all_sent("relay", both(GIVE, 4))
    all_sent("q", near)
    all_sent("sum", part.at[pl.ds(0, 14)])
    all_sent("state", held.at[pl.ds(0, 14)])
    for wave in range(len(WAVES)):
        all_sent(("out", wave), done[wave])
    for wave in range(len(WAVES)):
        receive(("out", wave), done[wave])
    assert len(send_ids) <= SENDS and len(ids) <= RECEIVES, (len(send_ids), len(ids))


SENDS = 14
RECEIVES = 72


def body(query_rows, key_rows, value_rows, out_weight):
    rows = [a.reshape(TOKENS * HEADS, SIZE) for a in (query_rows, key_rows, value_rows)]
    anywhere = pl.BlockSpec(memory_space=pltpu.HBM)
    result = pl.pallas_call(
        kernel,
        out_shape=pltpu.VMEM((TOKENS, WIDTH), BF16),
        in_specs=[anywhere] * 4,
        out_specs=pl.BlockSpec(memory_space=pltpu.VMEM),
        scratch_shapes=[pltpu.VMEM((2, WIDTH, columns), BF16) for columns in WAVES]
        + [pltpu.VMEM((ROWS, 2 * columns), F32) for columns in WAVES[-1:]]
        + [pltpu.VMEM((OWN, 2 * columns), BF16) for columns in WAVES]
        + [
            pltpu.VMEM((TOKENS * HEADS, SIZE), BF16),
            pltpu.VMEM((TOKENS * HEADS, SIZE), BF16),
            pltpu.VMEM((OWN * HEADS, SIZE), BF16),
            pltpu.VMEM((ROWS * PITCH, SIZE), F32),
            pltpu.VMEM((PAIRS, SUMS, SIZE), F32),
            pltpu.VMEM((8, SUMS, SIZE), F32),
            pltpu.VMEM((8, SUMS, SIZE), F32),
            pltpu.VMEM((PAIRS, SENT, SIZE), BF16),
            pltpu.VMEM((2, ROWS, WIDTH), BF16),
            pltpu.SemaphoreType.DMA((len(WAVES) + 3,)),
            pltpu.SemaphoreType.DMA((SENDS,)),
            pltpu.SemaphoreType.DMA((RECEIVES,)),
        ],
        compiler_params=pltpu.CompilerParams(
            collective_id=0, has_side_effects=True, vmem_limit_bytes=56 * 1024 * 1024
        ),
        name="attend",
    )(*rows, out_weight)
    return result.reshape(1, TOKENS, WIDTH)


def solution(mesh):
    placed = (
        P(("shift", "dp"), "sp", None, None),
        P(("shift", "dp"), "sp", None, None),
        P(("shift", "dp"), "sp", None, None),
        P(("shift", "dp"), None),
    )
    return jax.shard_map(
        body, mesh=mesh, in_specs=placed, out_specs=P(("shift", "dp"), "sp", None), check_vma=False
    )
```

time: 105 us -> 99.6 us (0.949)
  Pallas kernels: 104 us -> 98.2 us
    pallas_call x1, Pallas kernels: 104 us -> 98.2 us  [body(): pl.pallas_call(kernel, out_shape=pltpu.VMEM((TOKENS, WIDTH), BF16), in_sp...]
where the time goes in v3:
time: 99.6 us
  Pallas kernels  98.2 us (99%)
  local copies, waits for them, and re-layouts  1.32 us (1%)
    pallas_call x1, Pallas kernels, body(): pl.pallas_call(kernel, out_shape=pltpu.VMEM((TOKENS, WIDTH), BF16), in_sp...  98.2 us

profile of v3, /device:TPU:2, one launch (start us, length us, event | category | flops | bytes accessed | tf_op | source)
XLA Modules:
  0.0 99.6 jit_solution(11996604570200507177)
XLA Ops:
  0.0 98.2 %attend.1 = bf16[256,4096]{1,0:T(8,128)(2,1)S(1)} custom-call(bf16[8192,128]{1,0:T(8,128)(2,1)} %bitcast.5, bf16[8192,128]{1,0:T(8,128)(2,1)} %bitcast.6, bf16[8192,128]{1,0:T(8,128)(2,1)} %bitcast.7, bf16[256,4096]{1,0:T(8,128)(2,1)} %w_hbm.1), custom_call_target="tpu_custom_call" | custom-call | tf_op jit(solution)/shard_map/attend/pallas_call | solution.py:465
  98.2 1.3 %copy.6 = bf16[1,256,4096]{2,1,0:T(8,128)(2,1)} copy(bf16[1,256,4096]{2,1,0:T(8,128)(2,1)S(1)} %bitcast.4) | data formatting | bytes 4194304

commit v4 on v3

--- a/solution.py
+++ b/solution.py
@@ -1,3 +1,5 @@
+import functools
+
 import jax
 import jax.numpy as jnp
 from jax import lax
@@ -259,23 +261,11 @@
     widen(lambda row: k_in[pl.ds(row, HEADS), :], OWN, TOKENS, as_feature)
     widen_queries(0)
 
-    for d, u in ((1, 0), (-1, 1)):
-        reduce_add(d, 1, u)
-        reduce_send(d, 2, u)
-    gather_3(0, 0)
-    for step in (2, 3):
-        for u in (1, 0):
-            for d in (1, -1):
-                v = u if d == 1 else 1 - u
-                reduce_add(d, step, v)
-                reduce_send(d, step + 1, v)
-        if step == 2:
-            gather_2(0)
-            gather_1(1)
-        else:
-            send_queries(1)
-            gather_3(0, -1)
-            gather_3(1, 0)
+    def reduce_step(step, u):
+        for d in (1, -1):
+            v = u if d == 1 else 1 - u
+            reduce_add(d, step, v)
+            reduce_send(d, step + 1, v)
 
     def gather_send(d, step, u):
         ref = held.at[at(z - d * (step - 1), u)]
@@ -314,42 +304,33 @@
     def read_chunk(chunk):
         read_pairs(at(chunk, 0), 2, EARLY)
 
-    mine = at(z, 0)
-    for u in (0, 1):
-        for d in (1, -1):
-            receive(("sum", d, 4, u), lands[d].at[6 + u])
-        total = (part[mine + u] + from_left[6 + u] + from_right[6 + u]) * (1.0 / 2048.0)
-        held[mine + u, pl.ds(0, 2 * SIZE), :] = total[: 2 * SIZE].astype(BF16)
-        mass = total[2 * SIZE :]
-        high = mass.astype(BF16).astype(F32)
-        middle = (mass - high).astype(BF16).astype(F32)
-        low = mass - high - middle
-        terms = jnp.concatenate([high, middle, low, jnp.zeros_like(low)], axis=0)
-        held[mine + u, pl.ds(2 * SIZE, 32), :] = terms.astype(BF16)
-        for d in (1, -1):
-            gather_send(d, 1, u)
-
-    read_chunk(z)
-    gather_3(0, 1)
-    for step in (1, 2, 3):
+    def own_sums():
+        mine = at(z, 0)
         for u in (0, 1):
             for d in (1, -1):
-                gather_take(d, step, u)
-                if step < 3 or (u == 0) == (d == 1):
-                    gather_send(d, step + 1, u)
-        if step == 2:
-            gather_2(1)
-            gather_3(0, 2)
-            send_own(2)
-        if step == 3:
-            send_queries(2)
-            gather_3(1, -1)
-            gather_3(1, 1)
-        for d in (1, -1):
+                receive(("sum", d, 4, u), lands[d].at[6 + u])
+            total = (part[mine + u] + from_left[6 + u] + from_right[6 + u]) * (1.0 / 2048.0)
+            held[mine + u, pl.ds(0, 2 * SIZE), :] = total[: 2 * SIZE].astype(BF16)
+            mass = total[2 * SIZE :]
+            high = mass.astype(BF16).astype(F32)
+            middle = (mass - high).astype(BF16).astype(F32)
+            low = mass - high - middle
+            terms = jnp.concatenate([high, middle, low, jnp.zeros_like(low)], axis=0)
+            held[mine + u, pl.ds(2 * SIZE, 32), :] = terms.astype(BF16)
+            for d in (1, -1):
+                gather_send(d, 1, u)
+
+    def gather_step(step):
+        for u in (0, 1):
+            for d in (1, -1):
+                if step < 4 or (u == 0) == (d == 1):
+                    gather_take(d, step, u)
+                    if step < 3 or (step == 3 and (u == 0) == (d == 1)):
+                        gather_send(d, step + 1, u)
+
+    def read_step(step):
+        for d in (1, -1) if step < 4 else (1,):
             read_chunk(z - d * step)
-    gather_take(1, 4, 0)
-    gather_take(-1, 4, 1)
-    read_chunk(z + 4)
 
     def finish(wave):
         columns = pl.ds(pl.multiple_of(half * (WIDTH // 2) + columns_at(wave), 128), 2 * WAVES[wave])
@@ -363,12 +344,11 @@
             )
 
     def multiply(wave, rows_at, groups, first, last):
-        tile = 256 if WAVES[wave] % 256 == 0 else 128
-        for t in (0, 1):
-
-            def step(n, carry, t=t):
-                column = pl.multiple_of(n * tile, tile)
-                to = pl.multiple_of(t * WAVES[wave] + n * tile, tile)
+        for t in (0, 1):
+
+            def step(start, tile, n, carry, t=t):
+                column = pl.multiple_of(start + n * tile, tile)
+                to = pl.multiple_of(t * WAVES[wave] + start + n * tile, 128)
                 rows = pl.ds(rows_at, 256)
                 total = None if first else acc[rows, pl.ds(to, tile)]
                 for dg in groups:
@@ -387,7 +367,11 @@
                     out[:, pl.ds(at, tile)] = total.astype(BF16)
                 return carry
 
-            lax.fori_loop(0, WAVES[wave] // tile, step, 0)
+            pairs, rest = divmod(WAVES[wave], 256)
+            if pairs:
+                lax.fori_loop(0, pairs, functools.partial(step, 0, 256), 0)
+            if rest:
+                step(pairs * 256, rest, 0, 0)
 
     WHOLE = (0, -1, 1, 2)
 
@@ -398,48 +382,78 @@
     def own_products(wave):
         multiply(wave, OWN, WHOLE, True, True)
 
+    gather_3(0, 0)
+    for d, u in ((1, 0), (-1, 1)):
+        reduce_add(d, 1, u)
+        reduce_send(d, 2, u)
+    gather_1(1)
+    reduce_step(2, 1)
+    reduce_step(2, 0)
     send_own(3)
+    reduce_step(3, 1)
+    reduce_step(3, 0)
+    send_queries(2)
+    own_sums()
+    gather_2(1)
+    gather_3(1, 0)
+    gather_1(3)
+    gather_2(0)
     gather_3(1, 2)
+    gather_3(1, -1)
+    send_own(2)
+    read_chunk(z)
+    gather_step(1)
+    gather_3(1, 1)
+    send_queries(1)
+    gather_step(2)
+    gather_3(0, 1)
+    gather_1(2)
+    gather_step(3)
+    read_step(1)
+    gather_2(3)
+    gather_3(0, -1)
+    gather_3(0, 2)
+    read_step(2)
+    widen_queries(1)
+    widen_queries(2)
+    gather_4(1)
+    gather_3(3, -1)
+    read_step(3)
+    relay()
+    gather_step(4)
+    gather_3(3, 1)
+    send_own(4)
+    read_step(4)
+    own_products(1)
+    read_pairs(0, PAIRS, LATE)
+    near_products(1)
+    gather_3(2, 1)
+    gather_3(3, 0)
+    gather_3(3, 2)
     gather_4(0)
     own_products(0)
-    gather_1(2)
-    gather_4(1)
-    relay()
-    send_own(4)
-    widen_queries(1)
-    widen_queries(2)
-    read_pairs(0, PAIRS, LATE)
+    gather_1(4)
+    near_products(0)
+    gather_2(4)
+    gather_4(3)
+    gather_3(2, -1)
+    gather_2(2)
+    gather_3(4, 0)
     gather_3(2, 0)
-    gather_1(3)
-    gather_2(2)
-    near_products(0)
-    gather_3(3, 0)
-    gather_2(3)
-    gather_1(4)
-    near_products(1)
-    gather_3(2, -1)
-    gather_3(2, 1)
-    gather_3(3, -1)
-    gather_3(3, 1)
-    own_products(1)
-    gather_3(3, 2)
-    gather_3(4, 0)
-    gather_2(4)
+    gather_3(4, -1)
+    near_products(3)
+    own_products(3)
+    gather_3(4, 1)
+    gather_3(4, 2)
+    multiply(4, 0, (0, -1, 1), True, False)
+    gather_4(2)
     gather_3(2, 2)
-    gather_4(2)
     near_products(2)
-    gather_3(4, -1)
-    gather_3(4, 1)
     own_products(2)
-    gather_4(3)
-    near_products(3)
-    gather_3(4, 2)
-    own_products(3)
-    for rows_at in (0, OWN):
-        multiply(4, rows_at, (0, -1, 1), True, False)
     gather_4(4)
     multiply(4, 0, (2,), False, True)
     finish(4)
+    multiply(4, OWN, (0, -1, 1), True, False)
     multiply(4, OWN, (2,), False, True)
 
     for wave in range(len(WAVES)):

time: 99.6 us -> 98.3 us (0.987)
  Pallas kernels: 98.2 us -> 96.8 us
    pallas_call x1, Pallas kernels: 98.2 us -> 96.8 us  [body(): pl.pallas_call(kernel, out_shape=pltpu.VMEM((TOKENS, WIDTH), BF16), in_sp...]
where the time goes in v4:
time: 98.3 us; the launch traced here: 98.2 us
  Pallas kernels  96.8 us (98%)
  local copies, waits for them, and re-layouts  1.32 us (1%)
    pallas_call x1, Pallas kernels, body(): pl.pallas_call(kernel, out_shape=pltpu.VMEM((TOKENS, WIDTH), BF16), in_sp...  96.8 us

profile of v4, /device:TPU:2, one launch (start us, length us, event | category | flops | bytes accessed | tf_op | source)
XLA Modules:
  0.0 98.2 jit_solution(13178314106682021965)
XLA Ops:
  0.0 96.8 %attend.1 = bf16[256,4096]{1,0:T(8,128)(2,1)S(1)} custom-call(bf16[8192,128]{1,0:T(8,128)(2,1)} %bitcast.5, bf16[8192,128]{1,0:T(8,128)(2,1)} %bitcast.6, bf16[8192,128]{1,0:T(8,128)(2,1)} %bitcast.7, bf16[256,4096]{1,0:T(8,128)(2,1)} %w_hbm.1), custom_call_target="tpu_custom_call" | custom-call | tf_op jit(solution)/shard_map/attend/pallas_call | solution.py:479
  96.9 1.3 %copy.6 = bf16[1,256,4096]{2,1,0:T(8,128)(2,1)} copy(bf16[1,256,4096]{2,1,0:T(8,128)(2,1)S(1)} %bitcast.4) | data formatting | bytes 4194304

commit v5 on v4

--- a/solution.py
+++ b/solution.py
@@ -23,7 +23,7 @@
 GIVE, TAKE = 1, 2
 PAIRS = HEADS // 2
 SUMS = 2 * SIZE + 8
-SENT = 2 * SIZE + 32
+SENT = 2 * SIZE + 16
 F32 = jnp.float32
 BF16 = jnp.bfloat16
 
@@ -275,12 +275,12 @@
         receive(("state", d, step, u), held.at[at(z - d * step, u)])
 
     def read_pair(i, blocks):
-        terms = held[i, pl.ds(2 * SIZE, 32), :].astype(F32)
+        terms = held[i, pl.ds(2 * SIZE, 16), :].astype(F32)
         block_at = i
         other_at = (i % RING) * RING + i // RING
         for u in (0, 1):
             head = 2 * i + u
-            mass = terms[u : u + 1] + terms[8 + u : 9 + u] + terms[16 + u : 17 + u]
+            mass = terms[u : u + 1] + terms[2 + u : 3 + u] + terms[4 + u : 5 + u]
             state = held[i, pl.ds(u * SIZE, SIZE), :]
             for r, count in blocks:
                 ask = wide[pl.ds(r * PITCH + head, count, stride=PITCH), :]
@@ -315,8 +315,9 @@
             high = mass.astype(BF16).astype(F32)
             middle = (mass - high).astype(BF16).astype(F32)
             low = mass - high - middle
-            terms = jnp.concatenate([high, middle, low, jnp.zeros_like(low)], axis=0)
-            held[mine + u, pl.ds(2 * SIZE, 32), :] = terms.astype(BF16)
+            terms = high + pltpu.roll(middle, 2, axis=0) + pltpu.roll(low, 4, axis=0)
+            terms = jnp.concatenate([terms, jnp.zeros_like(low)], axis=0)
+            held[mine + u, pl.ds(2 * SIZE, 16), :] = terms.astype(BF16)
             for d in (1, -1):
                 gather_send(d, 1, u)
 

time: 98.3 us -> 98.3 us (level)
  no operation moved by 1% of the time
where the time goes in v5:
time: 98.3 us; the launch traced here: 98.2 us
  Pallas kernels  96.8 us (98%)
  local copies, waits for them, and re-layouts  1.32 us (1%)
    pallas_call x1, Pallas kernels, body(): pl.pallas_call(kernel, out_shape=pltpu.VMEM((TOKENS, WIDTH), BF16), in_sp...  96.8 us

profile of v5, /device:TPU:2, one launch (start us, length us, event | category | flops | bytes accessed | tf_op | source)
XLA Modules:
  0.0 98.2 jit_solution(8710241501318347455)
XLA Ops:
  0.0 96.8 %attend.1 = bf16[256,4096]{1,0:T(8,128)(2,1)S(1)} custom-call(bf16[8192,128]{1,0:T(8,128)(2,1)} %bitcast.5, bf16[8192,128]{1,0:T(8,128)(2,1)} %bitcast.6, bf16[8192,128]{1,0:T(8,128)(2,1)} %bitcast.7, bf16[256,4096]{1,0:T(8,128)(2,1)} %w_hbm.1), custom_call_target="tpu_custom_call" | custom-call | tf_op jit(solution)/shard_map/attend/pallas_call | solution.py:480
  96.9 1.3 %copy.6 = bf16[1,256,4096]{2,1,0:T(8,128)(2,1)} copy(bf16[1,256,4096]{2,1,0:T(8,128)(2,1)S(1)} %bitcast.4) | data formatting | bytes 4194304
